TPU v7x, 8 devices: a whole 2x2x1 slice. The times are simulated.
8 devices in a mesh: dp: 1 (over z), tp: 2 (over y), ep: 4 (over x, core).
Axes of the slice: x: 2, y: 2, z: 1, core: 2. Of those that a mesh axis runs over, the one named last changes fastest.
Arguments:
- tokens: bfloat16 [1024, 2304], P(('dp', 'ep', 'tp'))
- expert_ids: int32 [1024, 2], P(('dp', 'ep', 'tp'))
- gates: float32 [1024, 2], P(('dp', 'ep', 'tp'))
- w_gate: bfloat16 [8, 2304, 5760], P('ep', None, 'tp')
- w_up: bfloat16 [8, 2304, 5760], P('ep', None, 'tp')
- w_down: bfloat16 [8, 5760, 2304], P('ep', 'tp')
Outputs:
- output: bfloat16 [1024, 2304], P(('dp', 'ep', 'tp'))
All inputs are finite; a program needn't handle non-finite values.
Results may differ from a plain program's by a relative error of at most 0.001.
Values are sent between devices in bfloat16 or wider.
A program may use at most 1 GiB of HBM per device.

v0:
```python
import jax
import jax.numpy as jnp
from jax import lax
from jax.sharding import PartitionSpec as P


def solution(mesh):
    ep_size = mesh.shape["ep"]
    row_spec = P(("dp", "ep", "tp"), None)

    def local_layer(tokens, expert_ids, gates, w_gate, w_up, w_down):
        top_k = expert_ids.shape[1]
        local_experts = w_gate.shape[0]
        hidden = tokens.shape[1]
        all_tokens = lax.all_gather(tokens, ("ep", "tp"), tiled=True)
        all_ids = lax.all_gather(expert_ids, ("ep", "tp"), tiled=True)
        all_gates = lax.all_gather(gates, ("ep", "tp"), tiled=True)
        group_rows = all_tokens.shape[0]
        load = group_rows * top_k // (local_experts * ep_size)
        local_ids = all_ids.reshape(-1) - lax.axis_index("ep") * local_experts
        is_mine = (local_ids >= 0) & (local_ids < local_experts)
        sort_key = jnp.where(is_mine, local_ids, local_experts)
        order = jnp.argsort(sort_key, stable=True)[: local_experts * load].reshape(local_experts, load)
        row_index = order // top_k
        gate_disp = all_gates.reshape(-1)[order]
        x_disp = all_tokens[row_index]
        hidden_gate = jnp.einsum("ecd,edf->ecf", x_disp, w_gate, preferred_element_type=jnp.float32)
        hidden_up = jnp.einsum("ecd,edf->ecf", x_disp, w_up, preferred_element_type=jnp.float32)
        act_rows = (jax.nn.silu(hidden_gate) * hidden_up).astype(jnp.bfloat16)
        out_rows = jnp.einsum("ecf,efd->ecd", act_rows, w_down, preferred_element_type=jnp.float32)
        weighted = (out_rows * gate_disp[:, :, None]).reshape(-1, hidden)
        partial_sum = jax.ops.segment_sum(weighted, row_index.reshape(-1), num_segments=group_rows)
        own_rows = lax.psum_scatter(partial_sum, ("ep", "tp"), scatter_dimension=0, tiled=True)
        return own_rows.astype(jnp.bfloat16)

    return jax.shard_map(local_layer, mesh=mesh, in_specs=(row_spec, row_spec, row_spec, P("ep", None, "tp"), P("ep", None, "tp"), P("ep", "tp", None)), out_specs=row_spec, check_vma=False)
```

profile of v0, /device:TPU:0, one launch (start us, length us, event | category | flops | bytes accessed | tf_op | source)
XLA Modules:
  0.0 183.0 jit_solution(13581280085137432588)
XLA Ops:
  6.5 0.0 all-gather.2.cloned.1.call-start
  6.5 0.7 all-gather.2.cloned.1.call-update
  7.3 0.0 reduce-scatter.2.cloned.1.call-start
  7.3 13.6 %all_gather.11 = f32[1024,2]{0,1:T(2,128)S(1)} all-gather(f32[128,2]{0,1:T(2,128)} %param.8), channel_id=1, replica_groups=mesh['dp'=1,'tp'=2,'ep'=4] {'ep','tp'}, dimensions={0}, use_global_device_ids=true | all-gather | bytes 9216 | tf_op jit(solution)/shard_map/all_gather | solution.py:17
  20.9 0.2 copy.8
  21.1 0.3 reshape.19
  21.4 10.8 %all_gather.9 = s32[1024,2]{0,1:T(2,128)S(1)} all-gather(s32[128,2]{0,1:T(2,128)} %param.7), channel_id=1, replica_groups=mesh['dp'=1,'tp'=2,'ep'=4] {'ep','tp'}, dimensions={0}, use_global_device_ids=true | all-gather | bytes 9216 | tf_op jit(solution)/shard_map/all_gather | solution.py:16
  32.2 0.2 copy.7
  32.4 0.3 sub.17
  32.7 5.0 %sort.17 = (s32[2048]{0:T(1024)}, s32[2048]{0:T(1024)S(1)}) sort(s32[2048]{0:T(1024)S(1)} %and_select_fusion, s32[2048]{0:T(1024)S(1)} %iota.4), dimensions={0}, to_apply=%region_0.1 | sort | flops 22528 | bytes 32768 | tf_op jit(solution)/shard_map/jit(argsort)/sort | solution.py:23
  37.8 3.1 %gather_fusion.1 = f32[512]{0:T(512)S(1)} fusion(f32[2048]{0:T(1024)S(1)} %reshape.19, s32[1024]{0:T(1024)S(1)} %pad_clamp_fusion), kind=kCustom, calls=%fused_computation.1 | custom fusion | bytes 6144 | tf_op jit(solution)/shard_map/gather | solution.py:25
  41.0 4.0 %all-gather.2.cloned.1.call-done = bf16[1024,2304]{1,0:T(8,128)(2,1)} async-done(((bf16[128,2304]{1,0:T(8,128)(2,1)}), bf16[1024,2304]{1,0:T(8,128)(2,1)}) %all-gather.2.cloned.1.call-update) | async-done | bytes 4718608 | tf_op jit(solution)/shard_map/all_gather | solution.py:15
  45.0 7.8 %gather_fusion = bf16[512,2304]{1,0:T(8,128)(2,1)S(1)} fusion(bf16[1024,2304]{1,0:T(8,128)(2,1)} %all-gather.2.cloned.1.call-done, s32[1024]{0:T(1024)S(1)} %pad_clamp_fusion.1), kind=kCustom, calls=%fused_computation | custom fusion | bytes 4720640 | tf_op jit(solution)/shard_map/gather | solution.py:26
  52.9 14.7 %fusion.6 = f32[2,256,2880]{1,2,0:T(8,128)} fusion(bf16[2,256,2304]{2,1,0:T(8,128)(2,1)S(1)} %bitcast.15, bf16[2,2304,2880]{1,2,0:T(8,128)(2,1)} %param.9), kind=kOutput, calls=%fused_computation.21 | convolution fusion | flops 6794772480 | bytes 34799616 | tf_op jit(solution)/shard_map/ecd,edf->ecf/dot_general | solution.py:27
  67.6 25.6 %convolution_multiply_fusion = f32[2,256,2304]{2,1,0:T(8,128)} fusion(bf16[2,2880,2304]{2,1,0:T(8,128)(2,1)} %param.11, f32[2,256,2880]{1,2,0:T(8,128)} %fusion.6, bf16[2,256,2304]{2,1,0:T(8,128)(2,1)S(1)} %bitcast.16, bf16[2,2304,2880]{1,2,0:T(8,128)(2,1)} %param.10, f32[2,256]{1,0:T(2,128)S(1)} %reshape.30), kind=kOutput, calls=%fused_computation.6 | convolution fusion | flops 13599571968 | bytes 66062336 | tf_op jit(solution)/shard_map/ecf,efd->ecd/dot_general | solution.py:30
  93.2 13.2 %scatter_custom_fusion = f32[1024,2304]{1,0:T(8,128)} fusion(s32[512]{0:T(512)S(1)} %bitcast.20, f32[512,2304]{1,0:T(8,128)} %bitcast.21, f32[]{:T(128)} %constant.10.clone.1), kind=kCustom, calls=%fused_computation.4 | custom fusion | flops 1179648 | bytes 9437696 | tf_op jit(solution)/shard_map/scatter-add | solution.py:32
  106.4 0.0 reduce-scatter.2.cloned.1.call-update
  106.4 67.5 %reduce-scatter.2.cloned.1.call-done = f32[128,2304]{1,0:T(8,128)} async-done(((f32[1024,2304]{1,0:T(8,128)}), f32[128,2304]{1,0:T(8,128)}) %reduce-scatter.2.cloned.1.call-update) | async-done | bytes 1179664 | tf_op jit(solution)/shard_map/reduce_scatter | solution.py:33
  174.0 2.1 %convert_element_type.7 = bf16[128,2304]{1,0:T(8,128)(2,1)} convert(f32[128,2304]{1,0:T(8,128)} %reduce-scatter.2.cloned.1.call-done) | non-fusion elementwise | flops 294912 | bytes 1769472 | tf_op jit(solution)/shard_map/convert_element_type | solution.py:34
  (12 shorter events, 0.1 us)
Async XLA Ops:
  6.5 38.5 %all-gather.2.cloned.1.call-start = ((), (), s32[]{:S(2)}) async-start(), calls=%async_computation.1 | async-start | bytes 5308416 | tf_op jit(solution)/shard_map/all_gather | solution.py:15
  7.3 166.7 %reduce-scatter.2.cloned.1.call-start = ((), (), s32[]{:S(2)}) async-start(), calls=%async_computation.2 | async-start | bytes 10616832 | tf_op jit(solution)/shard_map/reduce_scatter | solution.py:33
Sparse Core Ops, SparseCore 0:
  9.1 35.8 all-gather.1
  106.6 67.3 reduce-scatter.1
where the time goes:
time: 183 us
  waiting for transfers between devices  72.3 us (40%)
  matrix products  40.3 us (22%)
  blocking collectives  24.4 us (13%)
  other arithmetic  20.4 us (11%)
  between operations  13.5 us (7%)
  local copies, waits for them, and re-layouts  12 us (7%)
    reduce_scatter x1, waiting for transfers between devices, local_layer(): lax.psum_scatter(partial_sum, ('ep', 'tp'), scatter_dimension=0, tiled=True)  67.5 us
    dot_general x1, matrix products, local_layer(): jnp.einsum('ecf,efd->ecd', act_rows, w_down, preferred_element_type=jnp.f...  25.6 us
    dot_general x1, matrix products, local_layer(): jnp.einsum('ecd,edf->ecf', x_disp, w_gate, preferred_element_type=jnp.flo...  14.7 us
    all_gather x1, blocking collectives, local_layer(): all_gates = lax.all_gather(gates, ('ep', 'tp'), tiled=True)  13.6 us
    scatter-add x1, other arithmetic, local_layer(): jax.ops.segment_sum(weighted, row_index.reshape(-1), num_segments=group_r...  13.2 us
    all_gather x1, blocking collectives, local_layer(): all_ids = lax.all_gather(expert_ids, ('ep', 'tp'), tiled=True)  10.8 us
    gather x1, local copies, waits for them, and re-layouts, local_layer(): x_disp = all_tokens[row_index]  7.83 us
    sort x1, other arithmetic, local_layer(): jnp.argsort(sort_key, stable=True)[:local_experts * load]  5.04 us
  transfers between devices with their start and end apart: 2, of which 2 were waited for; matrix products, arithmetic and copies ran while one was open for 5% of the time, Pallas kernels for 0%

commit v1 on v0

v1 whole, which is shorter than its diff:
```python
import functools

import jax
import jax.numpy as jnp
from jax import lax
from jax.experimental import pallas as pl
from jax.experimental.pallas import tpu as pltpu
from jax.sharding import PartitionSpec as P

MESH = pl.DeviceIdType.MESH
F32 = jnp.float32
BF16 = jnp.bfloat16

ROWS = 128
SLOTS = 64
KC = 256
CC = 256
WRING = 3
DRING = 2
LAG1, LAG2 = 1, 2


def f32dot(a, b):
    return jnp.dot(a, b, preferred_element_type=F32)


def split3(v):
    hi = v.astype(BF16)
    rest = v - hi.astype(F32)
    mid = rest.astype(BF16)
    low = (rest - mid.astype(F32)).astype(BF16)
    return jnp.concatenate([hi, mid, low], axis=1)


def sum3(v):
    n = v.shape[1] // 3
    return (v[:, 2 * n:] + v[:, n:2 * n]) + v[:, :n]


def chunks(total, size):
    return [(i, min(size, total - i)) for i in range(0, total, size)]


def kernel(meta_ref, tok_ref, wg_hbm, wu_hbm, wd_hbm, y_ref,
           meta_all, pack, slots, xs, wg_buf, wu_buf, wd_buf, acc_g, acc_u, h,
           perm, perm_t, merge, gcol, parts, o_a, o_b,
           a1, a2s, a2, b1, b2s, b2, own_b,
           meta_ss, meta_rs, d_ss, d_rs, w_sem, wd_sem,
           a1_ss, a1_rs, a2_ss, a2_rs, b1_ss, b1_rs, b2_ss, b2_rs):
    ep, tp = lax.axis_index("ep"), lax.axis_index("tp")
    core, x = lax.rem(ep, 2), lax.div(ep, 2)
    nk, ns = slots.shape[0], o_b.shape[0]
    ff = wg_buf.shape[3]

    def peer(rel):
        dx, dc, dy = rel // 4, (rel // 2) % 2, rel % 2
        return {"ep": lax.rem(x + dx, 2) * 2 + lax.rem(core + dc, 2), "tp": lax.rem(tp + dy, 2)}

    def ep_of(k):
        return lax.rem(x + k // 2, 2) * 2 + lax.rem(core + k % 2, 2)

    def w_copies(kc, slot):
        at = pl.ds(pl.multiple_of(kc * KC, KC), KC)
        return (pltpu.make_async_copy(wg_hbm.at[:, at, :], wg_buf.at[slot], w_sem.at[0, slot]),
                pltpu.make_async_copy(wu_hbm.at[:, at, :], wu_buf.at[slot], w_sem.at[1, slot]))

    def wd_copy(s, slot):
        at = pl.ds(pl.multiple_of(s * CC, CC), CC)
        return pltpu.make_async_copy(wd_hbm.at[:, :, at], wd_buf.at[slot], wd_sem.at[slot])

    def remote(src, dst, ss, rs, rel):
        return pltpu.make_async_remote_copy(src_ref=src, dst_ref=dst, send_sem=ss, recv_sem=rs,
                                            device_id=peer(rel), device_id_type=MESH)

    for i in range(WRING):
        for c in w_copies(i, i):
            c.start()
    for i in range(DRING):
        wd_copy(i, i).start()

    barrier = pltpu.get_barrier_semaphore()
    for rel in range(1, 8):
        pl.semaphore_signal(barrier, inc=1, device_id=peer(rel), device_id_type=MESH)
    pl.semaphore_wait(barrier, 7)

    def meta_copy(rel):
        return remote(meta_ref, meta_all.at[rel], meta_ss.at[rel], meta_rs.at[rel], rel)

    for rel in range(1, 8):
        meta_copy(rel).start()

    sub128 = lax.broadcasted_iota(jnp.int32, (ROWS, ROWS), 0)
    lane128 = lax.broadcasted_iota(jnp.int32, (ROWS, ROWS), 1)
    before = jnp.where(sub128 < lane128, 1.0, 0.0).astype(BF16)

    def select(meta, epv):
        lo = 2.0 * epv.astype(F32)
        id0, id1, g0, g1 = (meta[i:i + 1, :] for i in range(4))
        first = (id0 >= lo) & (id0 <= lo + 1.0)
        second = (id1 >= lo) & (id1 <= lo + 1.0)
        mask = jnp.where(first | second, 1.0, 0.0)
        local = jnp.where(first, id0 - lo, jnp.where(second, id1 - lo, 0.0))
        gate = jnp.where(first, g0, jnp.where(second, g1, 0.0))
        return mask, local, gate

    def ranks(masks):
        m = jnp.concatenate(masks + masks[:1] * (8 - len(masks)), axis=0)
        r = f32dot(m.astype(BF16), before)
        return jnp.where(m > 0.5, r, -1.0)

    slot_iota = lax.broadcasted_iota(jnp.int32, (SLOTS, ROWS), 0).astype(F32)
    own = ranks([select(meta_ref[...], ep_of(k))[0] for k in range(4)])
    pick = jnp.concatenate(
        [jnp.where(own[k:k + 1, :] == slot_iota, 1.0, 0.0) for k in range(4)], axis=0).astype(BF16)

    def d_copy(kc, rel):
        k = rel // 2
        return remote(pack.at[kc, pl.ds(k * SLOTS, SLOTS)], slots.at[kc, pl.ds(rel * SLOTS, SLOTS)],
                      d_ss.at[kc, rel], d_rs.at[kc, rel], rel)

    for kc in range(nk):
        pack[kc] = f32dot(pick, tok_ref[:, kc * KC:(kc + 1) * KC]).astype(BF16)
        slots[kc, 0:SLOTS] = pack[kc, 0:SLOTS]
        for rel in (7, 4, 5, 6, 1, 3, 2):
            d_copy(kc, rel).start()

    acc_g[...] = jnp.zeros_like(acc_g)
    acc_u[...] = jnp.zeros_like(acc_u)

    for rel in range(1, 8):
        meta_copy(rel).wait()
    meta_all[0] = meta_ref[...]

    chosen = [select(meta_all[rel], ep) for rel in range(8)]
    rank_in = ranks([c[0] for c in chosen])
    local_cols = []
    for rel in range(8):
        hit = rank_in[rel:rel + 1, :] == slot_iota
        local_cols.append(jnp.sum(jnp.where(hit, chosen[rel][1], 0.0), axis=1, keepdims=True))
        gcol[rel * SLOTS:(rel + 1) * SLOTS, :] = jnp.broadcast_to(
            jnp.sum(jnp.where(hit, chosen[rel][2], 0.0), axis=1, keepdims=True), (SLOTS, ROWS))
    nq = 8 * SLOTS
    local = jnp.concatenate([jnp.broadcast_to(c, (SLOTS, ROWS)) for c in local_cols], axis=0)
    q_sub = lax.broadcasted_iota(jnp.int32, (nq, nq), 0)
    q_lane = lax.broadcasted_iota(jnp.int32, (nq, nq), 1)
    after = jnp.where(q_sub > q_lane, 1.0, 0.0).astype(BF16)
    ones_before = f32dot(after, local.astype(BF16))
    q_col = lax.broadcasted_iota(jnp.int32, (nq, ROWS), 0).astype(F32)
    l_row = lax.broadcasted_iota(jnp.int32, (nq, ROWS), 1).astype(F32)
    place = jnp.where(local > 0.5, nq // 2 + ones_before, q_col - ones_before)
    diag = sub128 == lane128
    for j in range(nq // ROWS):
        at = slice(j * ROWS, (j + 1) * ROWS)
        perm_t[:, at] = jnp.where(place == l_row + float(j * ROWS), 1.0, 0.0).astype(BF16)
        row = jnp.sum(jnp.where(diag, place[at, :], 0.0), axis=0, keepdims=True)
        perm[:, at] = jnp.where(row == q_col, 1.0, 0.0).astype(BF16)

    s_lane = lane128.astype(F32)
    par = ranks([select(meta_all[1], ep_of(k))[0] for k in range(4)])
    for who, r in enumerate((own, par)):
        cols = [jnp.sum(jnp.where(diag, r[k:k + 1, :], 0.0), axis=1, keepdims=True) for k in range(4)]
        for j in range(2):
            hit = jnp.where(s_lane < float(SLOTS), cols[2 * j] - s_lane,
                            cols[2 * j + 1] - s_lane + float(SLOTS)) == 0.0
            merge[who, :, j * ROWS:(j + 1) * ROWS] = jnp.where(hit, 1.0, 0.0).astype(BF16)

    half = nq // 2

    def arrive(kc):
        slot = lax.rem(kc, WRING)
        for rel in range(1, 8):
            d_copy(kc, rel).wait_recv()
        xs[...] = f32dot(perm[...], slots[kc]).astype(BF16)
        for c in w_copies(kc, slot):
            c.wait()
        return slot

    def k_step(kc, carry):
        slot = arrive(kc)
        for e in range(2):
            xe = xs[e * half:(e + 1) * half, :]
            for n0, n in chunks(ff, 256):
                acc_g[e, :, n0:n0 + n] += f32dot(xe, wg_buf[slot, e, :, n0:n0 + n])
                acc_u[e, :, n0:n0 + n] += f32dot(xe, wu_buf[slot, e, :, n0:n0 + n])

        @pl.when(kc + WRING < nk)
        def _():
            for c in w_copies(kc + WRING, slot):
                c.start()

        return carry

    lax.fori_loop(0, nk - 1, k_step, 0)

    slot = arrive(nk - 1)
    for e in range(2):
        xe = xs[e * half:(e + 1) * half, :]
        for n0, n in chunks(ff, 256):
            a = acc_g[e, :, n0:n0 + n] + f32dot(xe, wg_buf[slot, e, :, n0:n0 + n])
            b = acc_u[e, :, n0:n0 + n] + f32dot(xe, wu_buf[slot, e, :, n0:n0 + n])
            h[e, :, n0:n0 + n] = (a * (1.0 / (1.0 + jnp.exp(-a))) * b).astype(BF16)

    hc = CC // 2

    def a1_copy(s):
        return remote(o_a.at[s, :, 1], a1.at[s], a1_ss.at[s], a1_rs.at[s], 1)

    def a2_copy(s, k):
        return remote(a2s.at[s, k], a2.at[s, k], a2_ss.at[s, k], a2_rs.at[s, k], 2 * k)

    def b1_copy(s, k):
        return remote(o_b.at[s, pl.ds(k * ROWS, ROWS)], b1.at[s, k], b1_ss.at[s, k], b1_rs.at[s, k], 2 * k)

    def b2_copy(s):
        return remote(b2s.at[s], b2.at[s], b2_ss.at[s], b2_rs.at[s], 1)

    def stage1(s):
        slot = lax.rem(s, DRING)
        wd_copy(s, slot).wait()
        for e in range(2):
            parts[e * half:(e + 1) * half, :] = split3(f32dot(h[e], wd_buf[slot, e]))
        for k in range(4):
            at = slice(k * ROWS, (k + 1) * ROWS)
            g = gcol[at, :]
            v = sum3(f32dot(perm_t[at, :], parts[...]))
            va, vb = v[:, :hc] * g, v[:, hc:] * g
            o_a[s, k, 0] = va[:SLOTS]
            o_a[s, k, 1] = va[SLOTS:]
            if k == 0:
                b1[s, 0] = vb
            else:
                o_b[s, at] = vb
        a1_copy(s).start()
        for k in (2, 3, 1):
            b1_copy(s, k).start()

        @pl.when(s + DRING < ns)
        def _():
            wd_copy(s + DRING, slot).start()

    def stage2(s):
        a1_copy(s).wait_recv()
        for k in (2, 3, 1, 0):
            t = o_a[s, k, 0] + a1[s, k]
            if k == 0:
                a2[s, 0] = t
            else:
                a2s[s, k] = t
                a2_copy(s, k).start()
        for k in range(1, 4):
            b1_copy(s, k).wait_recv()
        blocks = b1[s]
        v = blocks[:, SLOTS:, :].reshape(4 * SLOTS, hc)
        b2s[s] = sum3(f32dot(merge[1], split3(v)))
        b2_copy(s).start()
        v = blocks[:, :SLOTS, :].reshape(4 * SLOTS, hc)
        own_b[s] = sum3(f32dot(merge[0], split3(v)))

    def stage3(s):
        for k in range(1, 4):
            a2_copy(s, k).wait_recv()
        v = a2[s].reshape(4 * SLOTS, hc)
        ya = sum3(f32dot(merge[0], split3(v)))
        b2_copy(s).wait_recv()
        yb = own_b[s] + b2[s]
        at = pl.ds(pl.multiple_of(s * CC, CC), CC)
        y_ref[:, at] = jnp.concatenate([ya, yb], axis=1).astype(BF16)

    def s_step(s, carry):
        @pl.when(s < ns)
        def _():
            stage1(s)

        @pl.when((s >= LAG1) & (s < ns + LAG1))
        def _():
            stage2(s - LAG1)

        @pl.when(s >= LAG2)
        def _():
            stage3(s - LAG2)

        return carry

    lax.fori_loop(0, ns + LAG2, s_step, 0)

    def d_done(kc, carry):
        for rel in range(1, 8):
            d_copy(kc, rel).wait_send()
        return carry

    lax.fori_loop(0, nk, d_done, 0)

    def s_done(s, carry):
        a1_copy(s).wait_send()
        b2_copy(s).wait_send()
        for k in range(1, 4):
            a2_copy(s, k).wait_send()
            b1_copy(s, k).wait_send()
        return carry

    lax.fori_loop(0, ns, s_done, 0)


def solution(mesh):
    row_spec = P(("dp", "ep", "tp"), None)

    def local_layer(tokens, expert_ids, gates, w_gate, w_up, w_down):
        rows, hidden = tokens.shape
        ff = w_gate.shape[2]
        nk, ns = hidden // KC, hidden // CC
        nq, hc = 8 * SLOTS, CC // 2
        meta = jnp.concatenate(
            [expert_ids.T.astype(F32), gates.T, jnp.zeros((4, rows), F32)], axis=0)
        vm, dma = pltpu.VMEM, pltpu.SemaphoreType.DMA
        scratch = [
            vm((8, 8, rows), F32),
            vm((nk, 4 * SLOTS, KC), BF16),
            vm((nk, nq, KC), BF16),
            vm((nq, KC), BF16),
            vm((WRING, 2, KC, ff), BF16),
            vm((WRING, 2, KC, ff), BF16),
            vm((DRING, 2, ff, CC), BF16),
            vm((2, nq // 2, ff), F32),
            vm((2, nq // 2, ff), F32),
            vm((2, nq // 2, ff), BF16),
            vm((nq, nq), BF16),
            vm((nq, nq), BF16),
            vm((2, rows, 4 * SLOTS), BF16),
            vm((nq, ROWS), F32),
            vm((nq, 3 * CC), BF16),
            vm((ns, 4, 2, SLOTS, hc), F32),
            vm((ns, nq, hc), F32),
            vm((ns, 4, SLOTS, hc), F32),
            vm((ns, 4, SLOTS, hc), F32),
            vm((ns, 4, SLOTS, hc), F32),
            vm((ns, 4, ROWS, hc), F32),
            vm((ns, ROWS, hc), F32),
            vm((ns, ROWS, hc), F32),
            vm((ns, ROWS, hc), F32),
            dma((8,)), dma((8,)), dma((nk, 8)), dma((nk, 8)), dma((2, WRING)), dma((DRING,)),
            dma((ns,)), dma((ns,)), dma((ns, 4)), dma((ns, 4)),
            dma((ns, 4)), dma((ns, 4)), dma((ns,)), dma((ns,)),
        ]
        vmem = pl.BlockSpec(memory_space=pltpu.VMEM)
        hbm = pl.BlockSpec(memory_space=pl.ANY)
        return pl.pallas_call(
            kernel,
            out_shape=jax.ShapeDtypeStruct((rows, hidden), BF16),
            in_specs=[vmem, vmem, hbm, hbm, hbm],
            out_specs=vmem,
            scratch_shapes=scratch,
            compiler_params=pltpu.CompilerParams(
                collective_id=0, has_side_effects=True, vmem_limit_bytes=67_000_000),
        )(meta, tokens, w_gate, w_up, w_down)

    return jax.shard_map(
        local_layer, mesh=mesh,
        in_specs=(row_spec, row_spec, row_spec, P("ep", None, "tp"), P("ep", None, "tp"), P("ep", "tp", None)),
        out_specs=row_spec, check_vma=False)
```

time: 183 us -> 161 us (0.88); the launches traced: 183 us -> 159 us
  Pallas kernels: 0 us -> 83 us
  waiting for transfers between devices: 72.3 us -> 0 us
  local copies, waits for them, and re-layouts: 12 us -> 73.8 us
  matrix products: 40.3 us -> 0 us
  blocking collectives: 24.4 us -> 0 us
  other arithmetic: 20.4 us -> 2.02 us
  between operations: 13.5 us -> 0.01 us
    pallas_call x0 -> x1, Pallas kernels: none -> 83 us  [local_layer(): pl.pallas_call(kernel, out_shape=jax.ShapeDtypeStruct((rows, hidden), BF1...]
    unnamed x3, local copies, waits for them, and re-layouts: 0.01 us -> 73.7 us
    reduce_scatter x1 -> x0, waiting for transfers between devices: 67.5 us -> none  [local_layer(): lax.psum_scatter(partial_sum, ('ep', 'tp'), scatter_dimension=0, tiled=True)]
    dot_general x2 -> x0, matrix products: 40.3 us -> none  [the longest x1 25.6 us: local_layer(): jnp.einsum('ecf,efd->ecd', act_rows, w_down, preferred_element_type=jnp.f...]
    all_gather x2 -> x0, blocking collectives: 24.4 us -> none  [the longest x1 13.6 us: local_layer(): all_gates = lax.all_gather(gates, ('ep', 'tp'), tiled=True)]
    scatter-add x1 -> x0, other arithmetic: 13.2 us -> none  [local_layer(): jax.ops.segment_sum(weighted, row_index.reshape(-1), num_segments=group_r...]
    gather x3 -> x0, local copies, waits for them, and re-layouts: 11 us -> none  [the longest x1 7.83 us: local_layer(): x_disp = all_tokens[row_index]]
    sort x1 -> x0, other arithmetic: 5.04 us -> none  [local_layer(): jnp.argsort(sort_key, stable=True)[:local_experts * load]]
  transfers between devices with their start and end apart: 2 -> 0, of which waited for: 2 -> 0; matrix products, arithmetic and copies ran while one was open for 5% -> 0% of each run, Pallas kernels for 0% -> 0%
where the time goes in v1:
time: 161 us; the launch traced here: 159 us
  Pallas kernels  83 us (52%)
  local copies, waits for them, and re-layouts  73.8 us (46%)
  other arithmetic  2.02 us (1%)
    pallas_call x1, Pallas kernels, local_layer(): pl.pallas_call(kernel, out_shape=jax.ShapeDtypeStruct((rows, hidden), BF1...  83 us
    unnamed x3, local copies, waits for them, and re-layouts  73.7 us

profile of v1, /device:TPU:0, one launch (start us, length us, event | category | flops | bytes accessed | tf_op | source)
XLA Modules:
  0.0 158.8 jit_solution(15531993167491035658)
XLA Ops:
  0.0 0.1 pad.2.clone
  0.1 0.7 convert_bitcast_fusion
  0.8 1.3 maximum_maximum_fusion.meta_ref
  2.1 35.8 %copy.7.wg_hbm = bf16[2,2304,2880]{2,1,0:T(8,128)(2,1)} copy(bf16[2,2304,2880]{1,2,0:T(8,128)(2,1)} %param.9) | data formatting | bytes 53084160 | tf_op args[3]
  37.9 35.9 %copy.8.wu_hbm = bf16[2,2304,2880]{2,1,0:T(8,128)(2,1)} copy(bf16[2,2304,2880]{1,2,0:T(8,128)(2,1)} %param.10) | data formatting | bytes 53084160 | tf_op args[4]
  73.9 83.0 %shard_map.64 = bf16[128,2304]{1,0:T(8,128)(2,1)} custom-call(f32[8,128]{1,0:T(8,128)} %maximum_maximum_fusion.meta_ref, bf16[128,2304]{1,0:T(8,128)(2,1)} %tok_ref.1, bf16[2,2304,2880]{2,1,0:T(8,128)(2,1)} %copy.7.wg_hbm, bf16[2,2304,2880]{2,1,0:T(8,128)(2,1)} %copy.8.wu_hbm, bf16[2,2880,2304]{2,1,0:T(8,128)(2,1)} %wd_hbm.1), custom_call_target="tpu_custom_call" | custom-call | tf_op jit(solution)/shard_map/pallas_call | solution.py:346
  156.9 1.9 %copy.10 = bf16[128,2304]{1,0:T(8,128)(2,1)} copy(bf16[128,2304]{1,0:T(8,128)(2,1)} %shard_map.64) | data formatting | bytes 1179648
  (1 shorter events, 0.0 us)

commit v2 on v1

--- a/solution.py
+++ b/solution.py
@@ -16,12 +16,17 @@
 KC = 256
 CC = 256
 WRING = 3
+MC = 1440
 DRING = 2
 LAG1, LAG2 = 1, 2
 
 
 def f32dot(a, b):
     return jnp.dot(a, b, preferred_element_type=F32)
+
+
+def ntdot(a, b):
+    return lax.dot_general(a, b, (((1,), (1,)), ((), ())), preferred_element_type=F32)
 
 
 def split3(v):
@@ -41,16 +46,16 @@
     return [(i, min(size, total - i)) for i in range(0, total, size)]
 
 
-def kernel(meta_ref, tok_ref, wg_hbm, wu_hbm, wd_hbm, y_ref,
-           meta_all, pack, slots, xs, wg_buf, wu_buf, wd_buf, acc_g, acc_u, h,
+def kernel(ids_ref, gates_ref, tok_ref, wg_hbm, wu_hbm, wd_hbm, y_ref,
+           ids_all, gates_all, pack, slots, xs, wg_buf, wu_buf, wd_buf, acc_g, acc_u, h,
            perm, perm_t, merge, gcol, parts, o_a, o_b,
            a1, a2s, a2, b1, b2s, b2, own_b,
-           meta_ss, meta_rs, d_ss, d_rs, w_sem, wd_sem,
+           id_ss, id_rs, gate_ss, gate_rs, d_ss, d_rs, w_sem, wd_sem,
            a1_ss, a1_rs, a2_ss, a2_rs, b1_ss, b1_rs, b2_ss, b2_rs):
     ep, tp = lax.axis_index("ep"), lax.axis_index("tp")
     core, x = lax.rem(ep, 2), lax.div(ep, 2)
     nk, ns = slots.shape[0], o_b.shape[0]
-    ff = wg_buf.shape[3]
+    ff = wg_buf.shape[2]
 
     def peer(rel):
         dx, dc, dy = rel // 4, (rel // 2) % 2, rel % 2
@@ -61,8 +66,8 @@
 
     def w_copies(kc, slot):
         at = pl.ds(pl.multiple_of(kc * KC, KC), KC)
-        return (pltpu.make_async_copy(wg_hbm.at[:, at, :], wg_buf.at[slot], w_sem.at[0, slot]),
-                pltpu.make_async_copy(wu_hbm.at[:, at, :], wu_buf.at[slot], w_sem.at[1, slot]))
+        return (pltpu.make_async_copy(wg_hbm.at[:, :, at], wg_buf.at[slot], w_sem.at[0, slot]),
+                pltpu.make_async_copy(wu_hbm.at[:, :, at], wu_buf.at[slot], w_sem.at[1, slot]))
 
     def wd_copy(s, slot):
         at = pl.ds(pl.multiple_of(s * CC, CC), CC)
@@ -83,19 +88,22 @@
         pl.semaphore_signal(barrier, inc=1, device_id=peer(rel), device_id_type=MESH)
     pl.semaphore_wait(barrier, 7)
 
-    def meta_copy(rel):
-        return remote(meta_ref, meta_all.at[rel], meta_ss.at[rel], meta_rs.at[rel], rel)
+    def meta_copies(rel):
+        return (remote(ids_ref, ids_all.at[rel], id_ss.at[rel], id_rs.at[rel], rel),
+                remote(gates_ref, gates_all.at[rel], gate_ss.at[rel], gate_rs.at[rel], rel))
 
     for rel in range(1, 8):
-        meta_copy(rel).start()
+        for c in meta_copies(rel):
+            c.start()
 
     sub128 = lax.broadcasted_iota(jnp.int32, (ROWS, ROWS), 0)
     lane128 = lax.broadcasted_iota(jnp.int32, (ROWS, ROWS), 1)
     before = jnp.where(sub128 < lane128, 1.0, 0.0).astype(BF16)
 
-    def select(meta, epv):
+    def select(ids, gates, epv):
         lo = 2.0 * epv.astype(F32)
-        id0, id1, g0, g1 = (meta[i:i + 1, :] for i in range(4))
+        ids = ids.astype(F32)
+        id0, id1, g0, g1 = ids[0:1, :], ids[1:2, :], gates[0:1, :], gates[1:2, :]
         first = (id0 >= lo) & (id0 <= lo + 1.0)
         second = (id1 >= lo) & (id1 <= lo + 1.0)
         mask = jnp.where(first | second, 1.0, 0.0)
@@ -109,7 +117,7 @@
         return jnp.where(m > 0.5, r, -1.0)
 
     slot_iota = lax.broadcasted_iota(jnp.int32, (SLOTS, ROWS), 0).astype(F32)
-    own = ranks([select(meta_ref[...], ep_of(k))[0] for k in range(4)])
+    own = ranks([select(ids_ref[...], gates_ref[...], ep_of(k))[0] for k in range(4)])
     pick = jnp.concatenate(
         [jnp.where(own[k:k + 1, :] == slot_iota, 1.0, 0.0) for k in range(4)], axis=0).astype(BF16)
 
@@ -128,10 +136,12 @@
     acc_u[...] = jnp.zeros_like(acc_u)
 
     for rel in range(1, 8):
-        meta_copy(rel).wait()
-    meta_all[0] = meta_ref[...]
-
-    chosen = [select(meta_all[rel], ep) for rel in range(8)]
+        for c in meta_copies(rel):
+            c.wait()
+    ids_all[0] = ids_ref[...]
+    gates_all[0] = gates_ref[...]
+
+    chosen = [select(ids_all[rel], gates_all[rel], ep) for rel in range(8)]
     rank_in = ranks([c[0] for c in chosen])
     local_cols = []
     for rel in range(8):
@@ -156,7 +166,7 @@
         perm[:, at] = jnp.where(row == q_col, 1.0, 0.0).astype(BF16)
 
     s_lane = lane128.astype(F32)
-    par = ranks([select(meta_all[1], ep_of(k))[0] for k in range(4)])
+    par = ranks([select(ids_all[1], gates_all[1], ep_of(k))[0] for k in range(4)])
     for who, r in enumerate((own, par)):
         cols = [jnp.sum(jnp.where(diag, r[k:k + 1, :], 0.0), axis=1, keepdims=True) for k in range(4)]
         for j in range(2):
@@ -179,9 +189,10 @@
         slot = arrive(kc)
         for e in range(2):
             xe = xs[e * half:(e + 1) * half, :]
-            for n0, n in chunks(ff, 256):
-                acc_g[e, :, n0:n0 + n] += f32dot(xe, wg_buf[slot, e, :, n0:n0 + n])
-                acc_u[e, :, n0:n0 + n] += f32dot(xe, wu_buf[slot, e, :, n0:n0 + n])
+            for n0, n in chunks(ff, MC):
+                at = slice(n0, n0 + n)
+                acc_g[e, at, :] += ntdot(wg_buf[slot, e, at, :], xe)
+                acc_u[e, at, :] += ntdot(wu_buf[slot, e, at, :], xe)
 
         @pl.when(kc + WRING < nk)
         def _():
@@ -193,12 +204,16 @@
     lax.fori_loop(0, nk - 1, k_step, 0)
 
     slot = arrive(nk - 1)
+    eye = jnp.where(lax.broadcasted_iota(jnp.int32, (half, half), 0)
+                    == lax.broadcasted_iota(jnp.int32, (half, half), 1), 1.0, 0.0).astype(BF16)
     for e in range(2):
         xe = xs[e * half:(e + 1) * half, :]
         for n0, n in chunks(ff, 256):
-            a = acc_g[e, :, n0:n0 + n] + f32dot(xe, wg_buf[slot, e, :, n0:n0 + n])
-            b = acc_u[e, :, n0:n0 + n] + f32dot(xe, wu_buf[slot, e, :, n0:n0 + n])
-            h[e, :, n0:n0 + n] = (a * (1.0 / (1.0 + jnp.exp(-a))) * b).astype(BF16)
+            at = slice(n0, n0 + n)
+            a = acc_g[e, at, :] + ntdot(wg_buf[slot, e, at, :], xe)
+            b = acc_u[e, at, :] + ntdot(wu_buf[slot, e, at, :], xe)
+            act = (a * (1.0 / (1.0 + jnp.exp(-a))) * b).astype(BF16)
+            h[e, :, at] = ntdot(eye, act).astype(BF16)
 
     hc = CC // 2
 
@@ -309,19 +324,18 @@
         ff = w_gate.shape[2]
         nk, ns = hidden // KC, hidden // CC
         nq, hc = 8 * SLOTS, CC // 2
-        meta = jnp.concatenate(
-            [expert_ids.T.astype(F32), gates.T, jnp.zeros((4, rows), F32)], axis=0)
         vm, dma = pltpu.VMEM, pltpu.SemaphoreType.DMA
         scratch = [
-            vm((8, 8, rows), F32),
+            vm((8, 2, rows), jnp.int32),
+            vm((8, 2, rows), F32),
             vm((nk, 4 * SLOTS, KC), BF16),
             vm((nk, nq, KC), BF16),
             vm((nq, KC), BF16),
-            vm((WRING, 2, KC, ff), BF16),
-            vm((WRING, 2, KC, ff), BF16),
+            vm((WRING, 2, ff, KC), BF16),
+            vm((WRING, 2, ff, KC), BF16),
             vm((DRING, 2, ff, CC), BF16),
-            vm((2, nq // 2, ff), F32),
-            vm((2, nq // 2, ff), F32),
+            vm((2, ff, nq // 2), F32),
+            vm((2, ff, nq // 2), F32),
             vm((2, nq // 2, ff), BF16),
             vm((nq, nq), BF16),
             vm((nq, nq), BF16),
@@ -337,7 +351,7 @@
             vm((ns, ROWS, hc), F32),
             vm((ns, ROWS, hc), F32),
             vm((ns, ROWS, hc), F32),
-            dma((8,)), dma((8,)), dma((nk, 8)), dma((nk, 8)), dma((2, WRING)), dma((DRING,)),
+            dma((8,)), dma((8,)), dma((8,)), dma((8,)), dma((nk, 8)), dma((nk, 8)), dma((2, WRING)), dma((DRING,)),
             dma((ns,)), dma((ns,)), dma((ns, 4)), dma((ns, 4)),
             dma((ns, 4)), dma((ns, 4)), dma((ns,)), dma((ns,)),
         ]
@@ -346,12 +360,12 @@
         return pl.pallas_call(
             kernel,
             out_shape=jax.ShapeDtypeStruct((rows, hidden), BF16),
-            in_specs=[vmem, vmem, hbm, hbm, hbm],
+            in_specs=[vmem, vmem, vmem, hbm, hbm, hbm],
             out_specs=vmem,
             scratch_shapes=scratch,
             compiler_params=pltpu.CompilerParams(
                 collective_id=0, has_side_effects=True, vmem_limit_bytes=67_000_000),
-        )(meta, tokens, w_gate, w_up, w_down)
+        )(expert_ids.T, gates.T, tokens, w_gate.swapaxes(1, 2), w_up.swapaxes(1, 2), w_down)
 
     return jax.shard_map(
         local_layer, mesh=mesh,

time: 161 us -> 89 us (0.55); the launches traced: 159 us -> 88.9 us
  local copies, waits for them, and re-layouts: 73.8 us -> 1.92 us
  Pallas kernels: 83 us -> 87 us
  other arithmetic: 2.02 us -> 0 us
    unnamed x3 -> x1, local copies, waits for them, and re-layouts: 73.7 us -> 1.92 us
    pallas_call x1, Pallas kernels: 83 us -> 87 us  [local_layer(): pl.pallas_call(kernel, out_shape=jax.ShapeDtypeStruct((rows, hidden), BF1...]
where the time goes in v2:
time: 89 us; the launch traced here: 88.9 us
  Pallas kernels  87 us (98%)
  local copies, waits for them, and re-layouts  1.92 us (2%)
    pallas_call x1, Pallas kernels, local_layer(): pl.pallas_call(kernel, out_shape=jax.ShapeDtypeStruct((rows, hidden), BF1...  87 us
    unnamed x1, local copies, waits for them, and re-layouts  1.92 us

profile of v2, /device:TPU:0, one launch (start us, length us, event | category | flops | bytes accessed | tf_op | source)
XLA Modules:
  0.0 88.9 jit_solution(231532899331569181)
XLA Ops:
  0.0 87.0 %shard_map.64 = bf16[128,2304]{1,0:T(8,128)(2,1)} custom-call(s32[2,128]{1,0:T(2,128)} %bitcast.6, f32[2,128]{1,0:T(2,128)} %bitcast.7, bf16[128,2304]{1,0:T(8,128)(2,1)} %tok_ref.1, bf16[2,2880,2304]{2,1,0:T(8,128)(2,1)} %bitcast.4, bf16[2,2880,2304]{2,1,0:T(8,128)(2,1)} %bitcast.5, bf16[2,2880,2304]{2,1,0:T(8,128)(2,1)} %wd_hbm.1), custom_call_target="tpu_custom_call" | custom-call | tf_op jit(solution)/shard_map/pallas_call | solution.py:360
  87.0 1.9 %copy.8 = bf16[128,2304]{1,0:T(8,128)(2,1)} copy(bf16[128,2304]{1,0:T(8,128)(2,1)} %shard_map.64) | data formatting | bytes 1179648

commit v3 on v2

--- a/solution.py
+++ b/solution.py
@@ -16,6 +16,7 @@
 KC = 256
 CC = 256
 WRING = 3
+WFIRST = 1
 MC = 1440
 DRING = 2
 LAG1, LAG2 = 1, 2
@@ -47,8 +48,8 @@
 
 
 def kernel(ids_ref, gates_ref, tok_ref, wg_hbm, wu_hbm, wd_hbm, y_ref,
-           ids_all, gates_all, pack, slots, xs, wg_buf, wu_buf, wd_buf, acc_g, acc_u, h,
-           perm, perm_t, merge, gcol, parts, o_a, o_b,
+           ids_all, gates_all, pack, dense, repack, slots, xs, wg_buf, wu_buf, wd_buf, acc_g, acc_u, h,
+           pick_par, perm, perm_t, merge, gcol, parts, o_a, o_b,
            a1, a2s, a2, b1, b2s, b2, own_b,
            id_ss, id_rs, gate_ss, gate_rs, d_ss, d_rs, w_sem, wd_sem,
            a1_ss, a1_rs, a2_ss, a2_rs, b1_ss, b1_rs, b2_ss, b2_rs):
@@ -77,24 +78,17 @@
         return pltpu.make_async_remote_copy(src_ref=src, dst_ref=dst, send_sem=ss, recv_sem=rs,
                                             device_id=peer(rel), device_id_type=MESH)
 
-    for i in range(WRING):
-        for c in w_copies(i, i):
-            c.start()
-    for i in range(DRING):
-        wd_copy(i, i).start()
-
     barrier = pltpu.get_barrier_semaphore()
     for rel in range(1, 8):
         pl.semaphore_signal(barrier, inc=1, device_id=peer(rel), device_id_type=MESH)
-    pl.semaphore_wait(barrier, 7)
+    for i in range(WFIRST):
+        for c in w_copies(i, i):
+            c.start()
 
     def meta_copies(rel):
         return (remote(ids_ref, ids_all.at[rel], id_ss.at[rel], id_rs.at[rel], rel),
                 remote(gates_ref, gates_all.at[rel], gate_ss.at[rel], gate_rs.at[rel], rel))
 
-    for rel in range(1, 8):
-        for c in meta_copies(rel):
-            c.start()
 
     sub128 = lax.broadcasted_iota(jnp.int32, (ROWS, ROWS), 0)
     lane128 = lax.broadcasted_iota(jnp.int32, (ROWS, ROWS), 1)
@@ -118,19 +112,82 @@
 
     slot_iota = lax.broadcasted_iota(jnp.int32, (SLOTS, ROWS), 0).astype(F32)
     own = ranks([select(ids_ref[...], gates_ref[...], ep_of(k))[0] for k in range(4)])
-    pick = jnp.concatenate(
-        [jnp.where(own[k:k + 1, :] == slot_iota, 1.0, 0.0) for k in range(4)], axis=0).astype(BF16)
-
-    def d_copy(kc, rel):
-        k = rel // 2
-        return remote(pack.at[kc, pl.ds(k * SLOTS, SLOTS)], slots.at[kc, pl.ds(rel * SLOTS, SLOTS)],
-                      d_ss.at[kc, rel], d_rs.at[kc, rel], rel)
+
+    def picks(r):
+        return jnp.concatenate(
+            [jnp.where(r[k:k + 1, :] == slot_iota, 1.0, 0.0) for k in range(4)], axis=0).astype(BF16)
+
+    pick = picks(own)
+
+    def d_copy(kc, block, src, to):
+        return remote(src, slots.at[kc, pl.ds(block * SLOTS, SLOTS)],
+                      d_ss.at[kc, block], d_rs.at[kc, block], to)
+
+    def packed(kc, rel):
+        return d_copy(kc, rel, pack.at[kc, pl.ds(rel // 2 * SLOTS, SLOTS)], rel)
+
+    def handed(kc, block):
+        return d_copy(kc, block, slots.at[kc, pl.ds((block - 1) * SLOTS, SLOTS)], 1)
+
+    def repacked(kc, block):
+        return d_copy(kc, block, repack.at[lax.div(kc, 2), pl.ds(block // 2 * SLOTS, SLOTS)], block - 1)
+
+    def dense_copy(kc):
+        at = pl.ds(pl.multiple_of(kc * KC, KC), KC)
+        return remote(tok_ref.at[:, at], dense.at[lax.div(kc, 2)], d_ss.at[kc, 1], d_rs.at[kc, 1], 1)
+
+    def send(kc, way):
+        if way == "y":
+            dense_copy(kc).start()
+        for rel in {"x": (4, 6, 1, 3, 2), "y": (4, 6, 2), "direct": (7, 5, 4, 6, 1, 3, 2)}[way]:
+            packed(kc, rel).start()
+
+    def relay(kc, way):
+        if way == "x":
+            for block in (5, 7):
+                packed(kc, block - 1).wait_recv()
+                handed(kc, block).start()
+        else:
+            dense_copy(kc).wait_recv()
+            j = lax.div(kc, 2)
+            repack[j] = f32dot(pick_par[...], dense[j]).astype(BF16)
+            slots[kc, SLOTS:2 * SLOTS] = repack[j, 0:SLOTS]
+            for block in (5, 7, 3):
+                repacked(kc, block).start()
+
+    def take(kc, way):
+        for block in {"x": (1, 2, 3, 5, 7), "y": (2, 3, 4, 5, 6, 7), "direct": range(1, 8)}[way]:
+            packed(kc, block).wait_recv()
+
+    def sent(kc, way):
+        if way == "y":
+            dense_copy(kc).wait_send()
+        for block in range(2 if way == "y" else 1, 8):
+            packed(kc, block).wait_send()
+
+    def by_way(kc, act):
+        @pl.when(lax.rem(kc, 2) == 0)
+        def _():
+            act(kc, "x")
+
+        @pl.when(lax.rem(kc, 2) == 1)
+        def _():
+            act(kc, "y")
 
     for kc in range(nk):
         pack[kc] = f32dot(pick, tok_ref[:, kc * KC:(kc + 1) * KC]).astype(BF16)
         slots[kc, 0:SLOTS] = pack[kc, 0:SLOTS]
-        for rel in (7, 4, 5, 6, 1, 3, 2):
-            d_copy(kc, rel).start()
+    pl.semaphore_wait(barrier, 7)
+    for rel in range(1, 8):
+        for c in meta_copies(rel):
+            c.start()
+    for kc in range(3):
+        send(kc, "xy"[kc % 2])
+    for i in range(WFIRST, WRING):
+        for c in w_copies(i, i):
+            c.start()
+    for i in range(DRING):
+        wd_copy(i, i).start()
 
     acc_g[...] = jnp.zeros_like(acc_g)
     acc_u[...] = jnp.zeros_like(acc_u)
@@ -167,6 +224,7 @@
 
     s_lane = lane128.astype(F32)
     par = ranks([select(ids_all[1], gates_all[1], ep_of(k))[0] for k in range(4)])
+    pick_par[...] = picks(par)
     for who, r in enumerate((own, par)):
         cols = [jnp.sum(jnp.where(diag, r[k:k + 1, :], 0.0), axis=1, keepdims=True) for k in range(4)]
         for j in range(2):
@@ -178,14 +236,30 @@
 
     def arrive(kc):
         slot = lax.rem(kc, WRING)
-        for rel in range(1, 8):
-            d_copy(kc, rel).wait_recv()
         xs[...] = f32dot(perm[...], slots[kc]).astype(BF16)
         for c in w_copies(kc, slot):
             c.wait()
         return slot
 
+    last = nk - 1
+    for kc in range(3):
+        relay(kc, "xy"[kc % 2])
+        send(kc + 3, "xy"[(kc + 3) % 2])
+
     def k_step(kc, carry):
+        @pl.when((kc >= 1) & (kc + 2 < last))
+        def _():
+            by_way(kc + 2, relay)
+
+        @pl.when((kc >= 1) & (kc + 5 < last))
+        def _():
+            by_way(kc + 5, send)
+
+        @pl.when(kc + 3 == last)
+        def _():
+            send(last, "direct")
+
+        by_way(kc, take)
         slot = arrive(kc)
         for e in range(2):
             xe = xs[e * half:(e + 1) * half, :]
@@ -203,9 +277,8 @@
 
     lax.fori_loop(0, nk - 1, k_step, 0)
 
-    slot = arrive(nk - 1)
-    eye = jnp.where(lax.broadcasted_iota(jnp.int32, (half, half), 0)
-                    == lax.broadcasted_iota(jnp.int32, (half, half), 1), 1.0, 0.0).astype(BF16)
+    take(last, "direct")
+    slot = arrive(last)
     for e in range(2):
         xe = xs[e * half:(e + 1) * half, :]
         for n0, n in chunks(ff, 256):
@@ -213,7 +286,7 @@
             a = acc_g[e, at, :] + ntdot(wg_buf[slot, e, at, :], xe)
             b = acc_u[e, at, :] + ntdot(wu_buf[slot, e, at, :], xe)
             act = (a * (1.0 / (1.0 + jnp.exp(-a))) * b).astype(BF16)
-            h[e, :, at] = ntdot(eye, act).astype(BF16)
+            h[e, :, at] = act.T
 
     hc = CC // 2
 
@@ -299,11 +372,11 @@
     lax.fori_loop(0, ns + LAG2, s_step, 0)
 
     def d_done(kc, carry):
-        for rel in range(1, 8):
-            d_copy(kc, rel).wait_send()
+        by_way(kc, sent)
         return carry
 
-    lax.fori_loop(0, nk, d_done, 0)
+    lax.fori_loop(0, last, d_done, 0)
+    sent(last, "direct")
 
     def s_done(s, carry):
         a1_copy(s).wait_send()
@@ -329,6 +402,8 @@
             vm((8, 2, rows), jnp.int32),
             vm((8, 2, rows), F32),
             vm((nk, 4 * SLOTS, KC), BF16),
+            vm((nk // 2, rows, KC), BF16),
+            vm((nk // 2, 4 * SLOTS, KC), BF16),
             vm((nk, nq, KC), BF16),
             vm((nq, KC), BF16),
             vm((WRING, 2, ff, KC), BF16),
@@ -337,6 +412,7 @@
             vm((2, ff, nq // 2), F32),
             vm((2, ff, nq // 2), F32),
             vm((2, nq // 2, ff), BF16),
+            vm((4 * SLOTS, rows), BF16),
             vm((nq, nq), BF16),
             vm((nq, nq), BF16),
             vm((2, rows, 4 * SLOTS), BF16),

time: 89 us -> 83 us (0.933)
  Pallas kernels: 87 us -> 80.9 us
    pallas_call x1, Pallas kernels: 87 us -> 80.9 us  [local_layer(): pl.pallas_call(kernel, out_shape=jax.ShapeDtypeStruct((rows, hidden), BF1...]
where the time goes in v3:
time: 83 us; the launch traced here: 82.8 us
  Pallas kernels  80.9 us (97%)
  local copies, waits for them, and re-layouts  1.92 us (2%)
    pallas_call x1, Pallas kernels, local_layer(): pl.pallas_call(kernel, out_shape=jax.ShapeDtypeStruct((rows, hidden), BF1...  80.9 us
    unnamed x1, local copies, waits for them, and re-layouts  1.92 us

profile of v3, /device:TPU:0, one launch (start us, length us, event | category | flops | bytes accessed | tf_op | source)
XLA Modules:
  0.0 82.8 jit_solution(11407765807533807562)
XLA Ops:
  0.0 80.9 %shard_map.64 = bf16[128,2304]{1,0:T(8,128)(2,1)} custom-call(s32[2,128]{1,0:T(2,128)} %bitcast.6, f32[2,128]{1,0:T(2,128)} %bitcast.7, bf16[128,2304]{1,0:T(8,128)(2,1)} %tok_ref.1, bf16[2,2880,2304]{2,1,0:T(8,128)(2,1)} %bitcast.4, bf16[2,2880,2304]{2,1,0:T(8,128)(2,1)} %bitcast.5, bf16[2,2880,2304]{2,1,0:T(8,128)(2,1)} %wd_hbm.1), custom_call_target="tpu_custom_call" | custom-call | tf_op jit(solution)/shard_map/pallas_call | solution.py:436
  80.9 1.9 %copy.8 = bf16[128,2304]{1,0:T(8,128)(2,1)} copy(bf16[128,2304]{1,0:T(8,128)(2,1)} %shard_map.64) | data formatting | bytes 1179648

commit v4 on v3

--- a/solution.py
+++ b/solution.py
@@ -19,7 +19,10 @@
 WFIRST = 1
 MC = 1440
 DRING = 2
-LAG1, LAG2 = 1, 2
+LAG1, LAG2 = 3, 6
+AHEAD = 3
+RELAYS = 3
+RELAYED = 8
 
 
 def f32dot(a, b):
@@ -147,7 +150,7 @@
             for block in (5, 7):
                 packed(kc, block - 1).wait_recv()
                 handed(kc, block).start()
-        else:
+        if way == "y":
             dense_copy(kc).wait_recv()
             j = lax.div(kc, 2)
             repack[j] = f32dot(pick_par[...], dense[j]).astype(BF16)
@@ -165,14 +168,23 @@
         for block in range(2 if way == "y" else 1, 8):
             packed(kc, block).wait_send()
 
-    def by_way(kc, act):
-        @pl.when(lax.rem(kc, 2) == 0)
-        def _():
-            act(kc, "x")
-
-        @pl.when(lax.rem(kc, 2) == 1)
-        def _():
-            act(kc, "y")
+    last = nk - 1
+
+    def way_of(kc):
+        return "xy"[kc % 2] if kc < RELAYED else "direct"
+
+    def by_way(kc, act, ok=True):
+        if isinstance(kc, int):
+            act(kc, way_of(kc))
+            return
+        for i, way in enumerate(("x", "y")):
+            @pl.when((lax.rem(kc, 2) == i) & (kc < RELAYED) & ok)
+            def _():
+                act(kc, way)
+
+        @pl.when((kc >= RELAYED) & ok)
+        def _():
+            act(kc, "direct")
 
     for kc in range(nk):
         pack[kc] = f32dot(pick, tok_ref[:, kc * KC:(kc + 1) * KC]).astype(BF16)
@@ -181,8 +193,8 @@
     for rel in range(1, 8):
         for c in meta_copies(rel):
             c.start()
-    for kc in range(3):
-        send(kc, "xy"[kc % 2])
+    for kc in range(AHEAD):
+        by_way(kc, send)
     for i in range(WFIRST, WRING):
         for c in w_copies(i, i):
             c.start()
@@ -241,21 +253,18 @@
             c.wait()
         return slot
 
-    last = nk - 1
-    for kc in range(3):
-        relay(kc, "xy"[kc % 2])
-        send(kc + 3, "xy"[(kc + 3) % 2])
+    for kc in range(RELAYS):
+        by_way(kc, relay)
+        if kc + AHEAD < last:
+            by_way(kc + AHEAD, send)
 
     def k_step(kc, carry):
-        @pl.when((kc >= 1) & (kc + 2 < last))
-        def _():
-            by_way(kc + 2, relay)
-
-        @pl.when((kc >= 1) & (kc + 5 < last))
-        def _():
-            by_way(kc + 5, send)
-
-        @pl.when(kc + 3 == last)
+        later = kc + RELAYS - 1
+
+        by_way(later, relay, (kc >= 1) & (later < RELAYED))
+        by_way(later + AHEAD, send, (kc >= 1) & (later + AHEAD < last))
+
+        @pl.when(later == last - 1)
         def _():
             send(last, "direct")
 
@@ -275,9 +284,8 @@
 
         return carry
 
-    lax.fori_loop(0, nk - 1, k_step, 0)
-
-    take(last, "direct")
+    lax.fori_loop(0, last, k_step, 0)
+    by_way(last, take)
     slot = arrive(last)
     for e in range(2):
         xe = xs[e * half:(e + 1) * half, :]
@@ -375,8 +383,7 @@
         by_way(kc, sent)
         return carry
 
-    lax.fori_loop(0, last, d_done, 0)
-    sent(last, "direct")
+    lax.fori_loop(0, nk, d_done, 0)
 
     def s_done(s, carry):
         a1_copy(s).wait_send()
@@ -435,12 +442,12 @@
         hbm = pl.BlockSpec(memory_space=pl.ANY)
         return pl.pallas_call(
             kernel,
-            out_shape=jax.ShapeDtypeStruct((rows, hidden), BF16),
+            out_shape=pltpu.VMEM((rows, hidden), BF16),
             in_specs=[vmem, vmem, vmem, hbm, hbm, hbm],
             out_specs=vmem,
             scratch_shapes=scratch,
             compiler_params=pltpu.CompilerParams(
-                collective_id=0, has_side_effects=True, vmem_limit_bytes=67_000_000),
+                collective_id=0, has_side_effects=True, vmem_limit_bytes=61_000_000),
         )(expert_ids.T, gates.T, tokens, w_gate.swapaxes(1, 2), w_up.swapaxes(1, 2), w_down)
 
     return jax.shard_map(

time: 83 us -> 79.4 us (0.957)
  Pallas kernels: 80.9 us -> 78.4 us
  local copies, waits for them, and re-layouts: 1.92 us -> 0.82 us
    pallas_call x1, Pallas kernels: 80.9 us -> 78.4 us  [local_layer(): pl.pallas_call(kernel, out_shape=pltpu.VMEM((rows, hidden), BF16), in_spe...]
    unnamed x1, local copies, waits for them, and re-layouts: 1.92 us -> 0.82 us
where the time goes in v4:
time: 79.4 us; the launch traced here: 79.2 us
  Pallas kernels  78.4 us (99%)
  local copies, waits for them, and re-layouts  0.82 us (1%)
    pallas_call x1, Pallas kernels, local_layer(): pl.pallas_call(kernel, out_shape=pltpu.VMEM((rows, hidden), BF16), in_spe...  78.4 us

profile of v4, /device:TPU:0, one launch (start us, length us, event | category | flops | bytes accessed | tf_op | source)
XLA Modules:
  0.0 79.2 jit_solution(12717348790504602837)
XLA Ops:
  0.0 78.4 %shard_map.64 = bf16[128,2304]{1,0:T(8,128)(2,1)S(1)} custom-call(s32[2,128]{1,0:T(2,128)} %bitcast.6, f32[2,128]{1,0:T(2,128)} %bitcast.7, bf16[128,2304]{1,0:T(8,128)(2,1)} %tok_ref.1, bf16[2,2880,2304]{2,1,0:T(8,128)(2,1)} %bitcast.4, bf16[2,2880,2304]{2,1,0:T(8,128)(2,1)} %bitcast.5, bf16[2,2880,2304]{2,1,0:T(8,128)(2,1)} %wd_hbm.1), custom_call_target="tpu_custom_call" | custom-call | tf_op jit(solution)/shard_map/pallas_call | solution.py:443
  78.4 0.8 %copy.8 = bf16[128,2304]{1,0:T(8,128)(2,1)} copy(bf16[128,2304]{1,0:T(8,128)(2,1)S(1)} %shard_map.64) | data formatting | bytes 1179648

commit v5 on v4

--- a/solution.py
+++ b/solution.py
@@ -142,7 +142,7 @@
     def send(kc, way):
         if way == "y":
             dense_copy(kc).start()
-        for rel in {"x": (4, 6, 1, 3, 2), "y": (4, 6, 2), "direct": (7, 5, 4, 6, 1, 3, 2)}[way]:
+        for rel in {"x": (4, 6, 1, 3, 2), "y": (4, 6, 2), "direct": (4, 6, 1, 3, 2), "rest": (7, 5)}[way]:
             packed(kc, rel).start()
 
     def relay(kc, way):
@@ -264,9 +264,13 @@
         by_way(later, relay, (kc >= 1) & (later < RELAYED))
         by_way(later + AHEAD, send, (kc >= 1) & (later + AHEAD < last))
 
+        @pl.when(later == last - 2)
+        def _():
+            send(last, "direct")
+
         @pl.when(later == last - 1)
         def _():
-            send(last, "direct")
+            send(last, "rest")
 
         by_way(kc, take)
         slot = arrive(kc)

time: 79.4 us -> 79.3 us (level)
  no operation moved by 1% of the time
where the time goes in v5:
time: 79.3 us; the launch traced here: 79.2 us
  Pallas kernels  78.3 us (99%)
  local copies, waits for them, and re-layouts  0.82 us (1%)
    pallas_call x1, Pallas kernels, local_layer(): pl.pallas_call(kernel, out_shape=pltpu.VMEM((rows, hidden), BF16), in_spe...  78.3 us

profile of v5, /device:TPU:0, one launch (start us, length us, event | category | flops | bytes accessed | tf_op | source)
XLA Modules:
  0.0 79.2 jit_solution(5438863321821977016)
XLA Ops:
  0.0 78.3 %shard_map.64 = bf16[128,2304]{1,0:T(8,128)(2,1)S(1)} custom-call(s32[2,128]{1,0:T(2,128)} %bitcast.6, f32[2,128]{1,0:T(2,128)} %bitcast.7, bf16[128,2304]{1,0:T(8,128)(2,1)} %tok_ref.1, bf16[2,2880,2304]{2,1,0:T(8,128)(2,1)} %bitcast.4, bf16[2,2880,2304]{2,1,0:T(8,128)(2,1)} %bitcast.5, bf16[2,2880,2304]{2,1,0:T(8,128)(2,1)} %wd_hbm.1), custom_call_target="tpu_custom_call" | custom-call | tf_op jit(solution)/shard_map/pallas_call | solution.py:447
  78.4 0.8 %copy.8 = bf16[128,2304]{1,0:T(8,128)(2,1)} copy(bf16[128,2304]{1,0:T(8,128)(2,1)S(1)} %shard_map.64) | data formatting | bytes 1179648
